TPU v7x, 256 devices: a whole 4x4x8 slice. The times are simulated.
256 devices in a mesh: batch: 4 (over x), proto: 64 (over y, z, core).
Axes of the slice: x: 4, y: 4, z: 8, core: 2. Of those that a mesh axis runs over, the one named last changes fastest.
Arguments:
- view_codes: bfloat16 [4096, 1024], P('batch', 'proto'), may hold values from -80 to 80
- predictor_view_embeddings: bfloat16 [4096, 1024], P('batch', 'proto'), may hold values from -80 to 80
- prototypes: bfloat16 [65536, 1024], P('proto'), may hold values from -64 to 64
Outputs:
- assignments: bfloat16 [4096, 65536], P('batch', 'proto')
- loss_rows: float32 [4096], P('batch')
All inputs are finite; a program needn't handle non-finite values.
Results may differ from a plain program's by a relative error of at most 0.0034.
Values may be sent and summed in bfloat16 or wider, within the bound.
A program may use at most 64 MiB of HBM per device.

v0:
```python
import jax
import jax.numpy as jnp
from jax import lax
from jax.sharding import PartitionSpec as P

SINK_ITERS = 3
EPSILON = 0.05
SOFTMAX_TEMP_VALUE = 0.1


def copy_for_each(shard, axis):
    copies = jnp.broadcast_to(shard, (lax.axis_size(axis), *shard.shape))
    return lax.all_to_all(copies, axis, split_axis=0, concat_axis=0, tiled=True)


def of_everyone(shard, axis):
    return copy_for_each(shard, axis).sum(axis=0)


def together(arrays, axis):
    ravelled, at, gathered = (jnp.concatenate([a.reshape(-1) for a in arrays]), 0, [])
    subtotal = of_everyone(ravelled, axis)
    for a in arrays:
        gathered.append(subtotal[at : at + a.size].reshape(a.shape))
        at += a.size
    return tuple(gathered)


def normalized(prototypes):
    weights = prototypes.astype(jnp.float32)
    return (weights * lax.rsqrt(jnp.sum(weights * weights, axis=1, keepdims=True) + 1e-06)).astype(
        jnp.bfloat16
    )


def view_scores(embedded, unit_prototype_rows):
    products = jnp.dot(embedded, unit_prototype_rows.T, preferred_element_type=jnp.float32)
    values = embedded.astype(jnp.float32)
    inverse_factor = lax.rsqrt(jnp.sum(values * values, axis=1) + 1e-06)
    return products * inverse_factor[:, None]


def local(view_codes, predictor_view_embeddings, prototypes):
    unit_prototype_rows = normalized(prototypes)
    whole_first, whole_second = (
        lax.all_gather(view_codes, "proto", axis=1, tiled=True),
        lax.all_gather(predictor_view_embeddings, "proto", axis=1, tiled=True),
    )
    scores_codes = view_scores(whole_first, unit_prototype_rows)
    predictor_scores = view_scores(whole_second, unit_prototype_rows)
    kernel = jnp.exp(scores_codes / EPSILON)
    rows_total = kernel.shape[0] * lax.axis_size("batch")
    protos_total = kernel.shape[1] * lax.axis_size("proto")
    logit_scores = predictor_scores / SOFTMAX_TEMP_VALUE
    scale_rows = jnp.ones((kernel.shape[0],), jnp.float32)
    for iteration in range(SINK_ITERS):
        col_part = jnp.dot(scale_rows, kernel, precision=lax.Precision.HIGHEST)
        col_sums = of_everyone(col_part, "batch")
        scale_cols = 1.0 / (protos_total * col_sums)
        row_part = jnp.dot(kernel, scale_cols, precision=lax.Precision.HIGHEST)
        row_sums = of_everyone(row_part, "proto")
        scale_rows = 1.0 / (rows_total * row_sums)
    assign = kernel * scale_cols[None, :] * (rows_total * scale_rows)[:, None]
    assignments = (protos_total * assign).astype(jnp.bfloat16)
    cross_part = jnp.sum(assign * logit_scores, axis=1)
    totals, cross_term = together((jnp.sum(jnp.exp(logit_scores), axis=1), cross_part), "proto")
    loss_rows = jnp.log(totals) - cross_term
    return (assignments, loss_rows)


def solution(mesh):
    placed = (P("batch", "proto"), P("batch", "proto"), P("proto", None))
    return jax.shard_map(
        local,
        mesh=mesh,
        in_specs=placed,
        out_specs=(P("batch", "proto"), P("batch")),
        check_vma=False,
    )
```

profile of v0, /device:TPU:1, one launch (start us, length us, event | category | flops | bytes accessed | tf_op | source)
XLA Modules:
  0.0 249.5 jit_solution(1705991306893637967)
XLA Ops:
  8.7 2.1 fusion
  10.7 81.8 %all-gather.3.cloned.1.call-done = bf16[1024,1024]{0,1:T(8,128)(2,1)} async-done(((bf16[1024,16]{0,1:T(8,128)(2,1)}), bf16[1024,1024]{0,1:T(8,128)(2,1)}) %all-gather.3.cloned.1.call-update) | async-done | bytes 2097168 | tf_op jit(solution)/shard_map/all_gather | solution.py:46
  92.6 2.1 multiply_reduce_fusion.1
  94.7 4.0 %multiply_exponential_fusion = f32[1024,1024]{1,0:T(8,128)S(1)} fusion(bf16[1024,1024]{0,1:T(8,128)(2,1)} %all-gather.3.cloned.1.call-done, f32[1024]{0:T(1024)S(1)} %add_rsqrt_fusion.1, bf16[1024,1024]{1,0:T(8,128)(2,1)S(1)} %copy-done.1, f32[1024]{0:T(1024)S(1)} %add_rsqrt_fusion.2), kind=kOutput, calls=%fused_computation.25 | convolution fusion | flops 2152726528 | bytes 8396800 | tf_op jit(solution)/shard_map/dot_general | solution.py:37
  98.7 1.9 copy-done
  100.6 3.6 %fusion.14 = f32[1,1024]{1,0:T(1,128)S(1)} fusion(f32[1024,1024]{1,0:T(8,128)S(1)} %multiply_exponential_fusion), kind=kOutput, calls=%fused_computation.19 | convolution fusion | flops 12582912 | bytes 4198400 | tf_op jit(solution)/shard_map/dot_general | solution.py:57
  104.2 8.1 %all_to_all.42 = f32[4,1,1024]{2,1,0:T(1,128)S(1)} all-to-all(f32[4,1,1024]{2,1,0:T(1,128)S(1)} %broadcast_in_dim.26), channel_id=1, replica_groups=mesh['batch'=4,'proto'=64] {'batch'}, dimensions={0} | all-to-all | bytes 32768 | tf_op jit(solution)/shard_map/all_to_all | solution.py:13
  112.2 4.4 %fusion.12 = f32[1,1024]{1,0:T(1,128)S(1)} fusion(f32[1024,1]{0,1:T(1,128)S(1)} %bitcast.52, f32[1024,1024]{1,0:T(8,128)} %copy-done), kind=kOutput, calls=%fused_computation.17 | convolution fusion | flops 12582912 | bytes 4202496 | tf_op jit(solution)/shard_map/dot_general | solution.py:60
  116.8 19.7 %all_to_all.43 = f32[64,1,1024]{2,1,0:T(1,128)S(1)} all-to-all(f32[64,1,1024]{2,1,0:T(1,128)S(1)} %broadcast_in_dim.27), channel_id=1, replica_groups=mesh['batch'=4,'proto'=64] {'proto'}, dimensions={0} | all-to-all | bytes 524288 | tf_op jit(solution)/shard_map/all_to_all | solution.py:13
  136.7 5.6 %fusion.10 = f32[1,1024]{1,0:T(1,128)S(1)} fusion(f32[1024,1]{0,1:T(1,128)S(1)} %bitcast.53, f32[1024,1024]{1,0:T(8,128)} %copy-done), kind=kOutput, calls=%fused_computation.15 | convolution fusion | flops 12582912 | bytes 4202496 | tf_op jit(solution)/shard_map/dot_general | solution.py:57
  142.4 6.6 %all_to_all.44 = f32[4,1,1024]{2,1,0:T(1,128)S(1)} all-to-all(f32[4,1,1024]{2,1,0:T(1,128)S(1)} %broadcast_in_dim.28), channel_id=1, replica_groups=mesh['batch'=4,'proto'=64] {'batch'}, dimensions={0} | all-to-all | bytes 32768 | tf_op jit(solution)/shard_map/all_to_all | solution.py:13
  149.0 4.4 %fusion.8 = f32[1,1024]{1,0:T(1,128)S(1)} fusion(f32[1024,1]{0,1:T(1,128)S(1)} %bitcast.54, f32[1024,1024]{1,0:T(8,128)} %copy-done), kind=kOutput, calls=%fused_computation.13 | convolution fusion | flops 12582912 | bytes 4202496 | tf_op jit(solution)/shard_map/dot_general | solution.py:60
  153.6 19.1 %all_to_all.45 = f32[64,1,1024]{2,1,0:T(1,128)S(1)} all-to-all(f32[64,1,1024]{2,1,0:T(1,128)S(1)} %broadcast_in_dim.29), channel_id=1, replica_groups=mesh['batch'=4,'proto'=64] {'proto'}, dimensions={0} | all-to-all | bytes 524288 | tf_op jit(solution)/shard_map/all_to_all | solution.py:13
  172.8 5.6 %fusion.6 = f32[1,1024]{1,0:T(1,128)S(1)} fusion(f32[1024,1]{0,1:T(1,128)S(1)} %bitcast.55, f32[1024,1024]{1,0:T(8,128)} %copy-done), kind=kOutput, calls=%fused_computation.11 | convolution fusion | flops 12582912 | bytes 4202496 | tf_op jit(solution)/shard_map/dot_general | solution.py:57
  178.5 6.6 %all_to_all.46 = f32[4,1,1024]{2,1,0:T(1,128)S(1)} all-to-all(f32[4,1,1024]{2,1,0:T(1,128)S(1)} %broadcast_in_dim.30), channel_id=1, replica_groups=mesh['batch'=4,'proto'=64] {'batch'}, dimensions={0} | all-to-all | bytes 32768 | tf_op jit(solution)/shard_map/all_to_all | solution.py:13
  185.1 4.4 %fusion.4 = f32[1,1024]{1,0:T(1,128)S(1)} fusion(f32[1024,1]{0,1:T(1,128)S(1)} %bitcast.51, f32[1024,1024]{1,0:T(8,128)} %copy-done), kind=kOutput, calls=%fused_computation.8 | convolution fusion | flops 12582912 | bytes 4202496 | tf_op jit(solution)/shard_map/dot_general | solution.py:60
  190.4 7.9 %all-to-all-start.5 = ((f32[64,1,1024]{2,1,0:T(1,128)}), f32[64,1,1024]{2,1,0:T(1,128)S(1)}, u32[]{:S(2)}, u32[]{:S(2)}) async-start(f32[64,1,1024]{2,1,0:T(1,128)} %broadcast_in_dim.31), calls=%async_computation.5 | async-start | bytes 524288 | tf_op jit(solution)/shard_map/all_to_all | solution.py:13
  198.3 2.1 multiply_reduce_fusion
  200.4 9.9 %all-to-all-done.5 = f32[64,1,1024]{2,1,0:T(1,128)S(1)} async-done(((f32[64,1,1024]{2,1,0:T(1,128)}), f32[64,1,1024]{2,1,0:T(1,128)S(1)}, u32[]{:S(2)}, u32[]{:S(2)}) %all-to-all-start.5) | async-done | bytes 262176 | tf_op jit(solution)/shard_map/all_to_all | solution.py:13
  210.5 6.9 %fusion.2 = (f32[1024]{0:T(1024)S(1)}, f32[1024]{0:T(1024)S(1)}, bf16[1024,1024]{0,1:T(8,128)(2,1)}) fusion(f32[1024]{0:T(1024)S(1)} %add_rsqrt_fusion, f32[1024]{0:T(1024)S(1)} %divide_multiply_fusion, f32[1024]{0:T(1024)S(1)} %multiply_divide_fusion, f32[1024,1024]{1,0:T(8,128)} %copy-done, bf16[1024,1024]{0,1:T(8,128)(2,1)} %all-gather.5.cloned.1.call-done, ...), kind=kOutput, calls=%fused_computation.6 | convolution fusion | flops 2160064512 | bytes 10510336 | tf_op jit(solution)/shard_map/dot_general | solution.py:37
  217.3 1.1 broadcast_in_dim.32
  218.4 6.0 %all-to-all-start.6 = ((f32[64,1,2048]{2,1,0:T(1,128)}), f32[64,1,2048]{2,1,0:T(1,128)S(1)}, u32[]{:S(2)}, u32[]{:S(2)}) async-start(f32[64,1,2048]{2,1,0:T(1,128)} %broadcast_in_dim.32), calls=%async_computation.6 | async-start | bytes 1048576 | tf_op jit(solution)/shard_map/all_to_all | solution.py:13
  224.4 3.9 %copy.14 = bf16[1024,1024]{1,0:T(8,128)(2,1)} copy(bf16[1024,1024]{0,1:T(8,128)(2,1)} %get-tuple-element.10) | data formatting | bytes 4194304
  228.4 13.3 %all-to-all-done.6 = f32[64,1,2048]{2,1,0:T(1,128)S(1)} async-done(((f32[64,1,2048]{2,1,0:T(1,128)}), f32[64,1,2048]{2,1,0:T(1,128)S(1)}, u32[]{:S(2)}, u32[]{:S(2)}) %all-to-all-start.6) | async-done | bytes 524320 | tf_op jit(solution)/shard_map/all_to_all | solution.py:13
  (32 shorter events, 4.3 us)
Async XLA Ops:
  7.2 87.5 %copy-start.1 = (bf16[1024,1024]{1,0:T(8,128)(2,1)S(1)}, bf16[1024,1024]{1,0:T(8,128)(2,1)}, u32[]{:S(2)}) copy-start(bf16[1024,1024]{1,0:T(8,128)(2,1)} %param.5) | copy-start | bytes 6291460
  7.2 85.4 %all-gather.3.cloned.1.call-start = ((), (), s32[]{:S(2)}) async-start(), calls=%async_computation.7 | async-start | bytes 2129920 | tf_op jit(solution)/shard_map/all_gather | solution.py:46
  7.9 190.4 %all-gather.5.cloned.1.call-start = ((), (), s32[]{:S(2)}) async-start(), calls=%async_computation.8 | async-start | bytes 2129920 | tf_op jit(solution)/shard_map/all_gather | solution.py:47
  98.6 1.9 copy-start
  190.4 19.9 %all-to-all-start.5 = ((f32[64,1,1024]{2,1,0:T(1,128)}), f32[64,1,1024]{2,1,0:T(1,128)S(1)}, u32[]{:S(2)}, u32[]{:S(2)}) async-start(f32[64,1,1024]{2,1,0:T(1,128)} %broadcast_in_dim.31), calls=%async_computation.5 | async-start | bytes 524288 | tf_op jit(solution)/shard_map/all_to_all | solution.py:13
  218.4 23.3 %all-to-all-start.6 = ((f32[64,1,2048]{2,1,0:T(1,128)}), f32[64,1,2048]{2,1,0:T(1,128)S(1)}, u32[]{:S(2)}, u32[]{:S(2)}) async-start(f32[64,1,2048]{2,1,0:T(1,128)} %broadcast_in_dim.32), calls=%async_computation.6 | async-start | bytes 1048576 | tf_op jit(solution)/shard_map/all_to_all | solution.py:13
Sparse Core Ops, SparseCore 0:
  10.8 81.7 all-gather.2
  95.3 75.9 all-gather.4
where the time goes:
time: 250 us; the launch traced here: 249 us
  waiting for transfers between devices  106 us (42%)
  blocking collectives  59.9 us (24%)
  matrix products  39 us (16%)
  between operations  14.2 us (6%)
  starting transfers between devices  14 us (6%)
  local copies, waits for them, and re-layouts  8.12 us (3%)
  other arithmetic  7.8 us (3%)
    all_gather x1, waiting for transfers between devices, local(): lax.all_gather(view_codes, 'proto', axis=1, tiled=True)  81.8 us
    all_to_all x5, blocking collectives, copy_for_each(): return lax.all_to_all(copies, axis, split_axis=0, concat_axis=0, tiled=True)  59.9 us
    all_to_all x2, waiting for transfers between devices, copy_for_each(): return lax.all_to_all(copies, axis, split_axis=0, concat_axis=0, tiled=True)  23.2 us
    dot_general x3, matrix products, local(): col_part = jnp.dot(scale_rows, kernel, precision=lax.Precision.HIGHEST)  14.9 us
    all_to_all x2, starting transfers between devices, copy_for_each(): return lax.all_to_all(copies, axis, split_axis=0, concat_axis=0, tiled=True)  13.9 us
    dot_general x3, matrix products, local(): row_part = jnp.dot(kernel, scale_cols, precision=lax.Precision.HIGHEST)  13.3 us
    dot_general x2, matrix products, view_scores(): jnp.dot(embedded, unit_prototype_rows.T, preferred_element_type=jnp.float32)  10.9 us
    unnamed x5, local copies, waits for them, and re-layouts  5.86 us
  transfers between devices with their start and end apart: 4, of which 3 were waited for; matrix products, arithmetic and copies ran while one was open for 18% of the time, Pallas kernels for 0%

commit v1 on v0

--- a/solution.py
+++ b/solution.py
@@ -1,3 +1,4 @@
+import functools
 import jax
 import jax.numpy as jnp
 from jax import lax
@@ -6,6 +7,19 @@
 SINK_ITERS = 3
 EPSILON = 0.05
 SOFTMAX_TEMP_VALUE = 0.1
+
+
+def define_notes(inputs, device_axis):
+    n_slots = lax.axis_size(device_axis)
+    grid = []
+    for s in range(inputs.ndim):
+        grid.append(n_slots if s == 1 else 1)
+    return lax.all_to_all(
+        jnp.tile(inputs, grid), axis_name=device_axis, split_axis=1, concat_axis=1, tiled=True
+    )
+
+
+press_cells = functools.partial(define_notes, device_axis="proto")
 
 
 def copy_for_each(shard, axis):
@@ -43,7 +57,7 @@
 def local(view_codes, predictor_view_embeddings, prototypes):
     unit_prototype_rows = normalized(prototypes)
     whole_first, whole_second = (
-        lax.all_gather(view_codes, "proto", axis=1, tiled=True),
+        press_cells(view_codes),
         lax.all_gather(predictor_view_embeddings, "proto", axis=1, tiled=True),
     )
     scores_codes = view_scores(whole_first, unit_prototype_rows)

time: 250 us -> 230 us (0.920)
  waiting for transfers between devices: 106 us -> 73.5 us
  starting transfers between devices: 14 us -> 26.6 us
    all_gather x1 -> x0, waiting for transfers between devices: 81.8 us -> none  [local(): lax.all_gather(view_codes, 'proto', axis=1, tiled=True)]
    all_to_all x0 -> x1, waiting for transfers between devices: none -> 49.6 us  [define_notes(): lax.all_to_all(jnp.tile(inputs, grid), axis_name=device_axis, split_axis=...]
    all_to_all x0 -> x1, starting transfers between devices: none -> 13.1 us  [define_notes(): lax.all_to_all(jnp.tile(inputs, grid), axis_name=device_axis, split_axis=...]
where the time goes in v1:
time: 230 us; the launch traced here: 229 us
  waiting for transfers between devices  73.5 us (32%)
  blocking collectives  59.3 us (26%)
  matrix products  39 us (17%)
  starting transfers between devices  26.6 us (12%)
  between operations  14.2 us (6%)
  local copies, waits for them, and re-layouts  10.5 us (5%)
  other arithmetic  6.21 us (3%)
    all_to_all x5, blocking collectives, copy_for_each(): return lax.all_to_all(copies, axis, split_axis=0, concat_axis=0, tiled=True)  59.3 us
    all_to_all x1, waiting for transfers between devices, define_notes(): lax.all_to_all(jnp.tile(inputs, grid), axis_name=device_axis, split_axis=...  49.6 us
    all_to_all x2, waiting for transfers between devices, copy_for_each(): return lax.all_to_all(copies, axis, split_axis=0, concat_axis=0, tiled=True)  23.2 us
    dot_general x3, matrix products, local(): col_part = jnp.dot(scale_rows, kernel, precision=lax.Precision.HIGHEST)  14.9 us
    all_to_all x2, starting transfers between devices, copy_for_each(): return lax.all_to_all(copies, axis, split_axis=0, concat_axis=0, tiled=True)  13.4 us
    dot_general x3, matrix products, local(): row_part = jnp.dot(kernel, scale_cols, precision=lax.Precision.HIGHEST)  13.3 us
    all_to_all x1, starting transfers between devices, define_notes(): lax.all_to_all(jnp.tile(inputs, grid), axis_name=device_axis, split_axis=...  13.1 us
    dot_general x2, matrix products, view_scores(): jnp.dot(embedded, unit_prototype_rows.T, preferred_element_type=jnp.float32)  10.9 us
  transfers between devices with their start and end apart: 4, of which 3 were waited for; matrix products, arithmetic and copies ran while one was open for 18% of the time, Pallas kernels for 0%

profile of v1, /device:TPU:1, one launch (start us, length us, event | category | flops | bytes accessed | tf_op | source)
XLA Modules:
  0.0 229.3 jit_solution(16280516851337928532)
XLA Ops:
  7.2 2.3 %tile.2 = bf16[1024,64,16]{0,2,1:T(8,128)(2,1)} broadcast(bf16[1024,16]{0,1:T(8,128)(2,1)} %param.3), dimensions={0,2} | broadcast | bytes 2129920 | tf_op jit(solution)/shard_map/tile | solution.py:18
  9.5 13.1 %all-to-all-start = ((bf16[1024,64,16]{0,2,1:T(8,128)(2,1)}), bf16[1024,64,16]{0,2,1:T(8,128)(2,1)S(1)}, u32[]{:S(2)}, u32[]{:S(2)}) async-start(bf16[1024,64,16]{0,2,1:T(8,128)(2,1)} %tile.2), calls=%async_computation | async-start | bytes 4194304 | tf_op jit(solution)/shard_map/all_to_all | solution.py:17
  23.4 2.1 fusion
  25.5 49.6 %all-to-all-done = bf16[1024,64,16]{0,2,1:T(8,128)(2,1)S(1)} async-done(((bf16[1024,64,16]{0,2,1:T(8,128)(2,1)}), bf16[1024,64,16]{0,2,1:T(8,128)(2,1)S(1)}, u32[]{:S(2)}, u32[]{:S(2)}) %all-to-all-start) | async-done | bytes 2097184 | tf_op jit(solution)/shard_map/all_to_all | solution.py:17
  75.5 4.0 %multiply_exponential_fusion = f32[1024,1024]{1,0:T(8,128)S(1)} fusion(bf16[1024,1024]{0,1:T(8,128)(2,1)S(1)} %bitcast.46, f32[1024]{0:T(1024)S(1)} %add_rsqrt_fusion.1, bf16[1024,1024]{1,0:T(8,128)(2,1)} %param.5, f32[1024]{0:T(1024)S(1)} %add_rsqrt_fusion.2), kind=kOutput, calls=%fused_computation.25 | convolution fusion | flops 2152726528 | bytes 8396800 | tf_op jit(solution)/shard_map/dot_general | solution.py:51
  79.5 1.9 copy-done
  81.5 3.6 %fusion.14 = f32[1,1024]{1,0:T(1,128)S(1)} fusion(f32[1024,1024]{1,0:T(8,128)S(1)} %multiply_exponential_fusion), kind=kOutput, calls=%fused_computation.19 | convolution fusion | flops 12582912 | bytes 4198400 | tf_op jit(solution)/shard_map/dot_general | solution.py:71
  85.0 8.0 %all_to_all.51 = f32[4,1,1024]{2,1,0:T(1,128)S(1)} all-to-all(f32[4,1,1024]{2,1,0:T(1,128)S(1)} %broadcast_in_dim.26), channel_id=1, replica_groups=mesh['batch'=4,'proto'=64] {'batch'}, dimensions={0} | all-to-all | bytes 32768 | tf_op jit(solution)/shard_map/all_to_all | solution.py:27
  93.1 4.4 %fusion.12 = f32[1,1024]{1,0:T(1,128)S(1)} fusion(f32[1024,1]{0,1:T(1,128)S(1)} %bitcast.54, f32[1024,1024]{1,0:T(8,128)} %copy-done), kind=kOutput, calls=%fused_computation.17 | convolution fusion | flops 12582912 | bytes 4202496 | tf_op jit(solution)/shard_map/dot_general | solution.py:74
  97.7 19.1 %all_to_all.52 = f32[64,1,1024]{2,1,0:T(1,128)S(1)} all-to-all(f32[64,1,1024]{2,1,0:T(1,128)S(1)} %broadcast_in_dim.27), channel_id=1, replica_groups=mesh['batch'=4,'proto'=64] {'proto'}, dimensions={0} | all-to-all | bytes 524288 | tf_op jit(solution)/shard_map/all_to_all | solution.py:27
  116.9 5.6 %fusion.10 = f32[1,1024]{1,0:T(1,128)S(1)} fusion(f32[1024,1]{0,1:T(1,128)S(1)} %bitcast.55, f32[1024,1024]{1,0:T(8,128)} %copy-done), kind=kOutput, calls=%fused_computation.15 | convolution fusion | flops 12582912 | bytes 4202496 | tf_op jit(solution)/shard_map/dot_general | solution.py:71
  122.6 6.6 %all_to_all.53 = f32[4,1,1024]{2,1,0:T(1,128)S(1)} all-to-all(f32[4,1,1024]{2,1,0:T(1,128)S(1)} %broadcast_in_dim.28), channel_id=1, replica_groups=mesh['batch'=4,'proto'=64] {'batch'}, dimensions={0} | all-to-all | bytes 32768 | tf_op jit(solution)/shard_map/all_to_all | solution.py:27
  129.2 4.4 %fusion.8 = f32[1,1024]{1,0:T(1,128)S(1)} fusion(f32[1024,1]{0,1:T(1,128)S(1)} %bitcast.56, f32[1024,1024]{1,0:T(8,128)} %copy-done), kind=kOutput, calls=%fused_computation.13 | convolution fusion | flops 12582912 | bytes 4202496 | tf_op jit(solution)/shard_map/dot_general | solution.py:74
  133.8 19.0 %all_to_all.54 = f32[64,1,1024]{2,1,0:T(1,128)S(1)} all-to-all(f32[64,1,1024]{2,1,0:T(1,128)S(1)} %broadcast_in_dim.29), channel_id=1, replica_groups=mesh['batch'=4,'proto'=64] {'proto'}, dimensions={0} | all-to-all | bytes 524288 | tf_op jit(solution)/shard_map/all_to_all | solution.py:27
  152.9 5.6 %fusion.6 = f32[1,1024]{1,0:T(1,128)S(1)} fusion(f32[1024,1]{0,1:T(1,128)S(1)} %bitcast.57, f32[1024,1024]{1,0:T(8,128)} %copy-done), kind=kOutput, calls=%fused_computation.11 | convolution fusion | flops 12582912 | bytes 4202496 | tf_op jit(solution)/shard_map/dot_general | solution.py:71
  158.6 6.7 %all_to_all.55 = f32[4,1,1024]{2,1,0:T(1,128)S(1)} all-to-all(f32[4,1,1024]{2,1,0:T(1,128)S(1)} %broadcast_in_dim.30), channel_id=1, replica_groups=mesh['batch'=4,'proto'=64] {'batch'}, dimensions={0} | all-to-all | bytes 32768 | tf_op jit(solution)/shard_map/all_to_all | solution.py:27
  165.3 4.4 %fusion.4 = f32[1,1024]{1,0:T(1,128)S(1)} fusion(f32[1024,1]{0,1:T(1,128)S(1)} %bitcast.53, f32[1024,1024]{1,0:T(8,128)} %copy-done), kind=kOutput, calls=%fused_computation.8 | convolution fusion | flops 12582912 | bytes 4202496 | tf_op jit(solution)/shard_map/dot_general | solution.py:74
  170.6 7.4 %all-to-all-start.6 = ((f32[64,1,1024]{2,1,0:T(1,128)}), f32[64,1,1024]{2,1,0:T(1,128)S(1)}, u32[]{:S(2)}, u32[]{:S(2)}) async-start(f32[64,1,1024]{2,1,0:T(1,128)} %broadcast_in_dim.31), calls=%async_computation.6 | async-start | bytes 524288 | tf_op jit(solution)/shard_map/all_to_all | solution.py:27
  178.0 2.1 multiply_reduce_fusion
  180.1 9.9 %all-to-all-done.6 = f32[64,1,1024]{2,1,0:T(1,128)S(1)} async-done(((f32[64,1,1024]{2,1,0:T(1,128)}), f32[64,1,1024]{2,1,0:T(1,128)S(1)}, u32[]{:S(2)}, u32[]{:S(2)}) %all-to-all-start.6) | async-done | bytes 262176 | tf_op jit(solution)/shard_map/all_to_all | solution.py:27
  190.2 6.9 %fusion.2 = (f32[1024]{0:T(1024)S(1)}, f32[1024]{0:T(1024)S(1)}, bf16[1024,1024]{0,1:T(8,128)(2,1)}) fusion(f32[1024]{0:T(1024)S(1)} %add_rsqrt_fusion, f32[1024]{0:T(1024)S(1)} %divide_multiply_fusion, f32[1024]{0:T(1024)S(1)} %multiply_divide_fusion, f32[1024,1024]{1,0:T(8,128)} %copy-done, bf16[1024,1024]{0,1:T(8,128)(2,1)} %all-gather.2.cloned.1.call-done, ...), kind=kOutput, calls=%fused_computation.6 | convolution fusion | flops 2160064512 | bytes 10510336 | tf_op jit(solution)/shard_map/dot_general | solution.py:51
  198.2 6.0 %all-to-all-start.7 = ((f32[64,1,2048]{2,1,0:T(1,128)}), f32[64,1,2048]{2,1,0:T(1,128)S(1)}, u32[]{:S(2)}, u32[]{:S(2)}) async-start(f32[64,1,2048]{2,1,0:T(1,128)} %broadcast_in_dim.32), calls=%async_computation.7 | async-start | bytes 1048576 | tf_op jit(solution)/shard_map/all_to_all | solution.py:27
  204.2 3.9 %copy.16 = bf16[1024,1024]{1,0:T(8,128)(2,1)} copy(bf16[1024,1024]{0,1:T(8,128)(2,1)} %get-tuple-element.12) | data formatting | bytes 4194304
  208.2 13.3 %all-to-all-done.7 = f32[64,1,2048]{2,1,0:T(1,128)S(1)} async-done(((f32[64,1,2048]{2,1,0:T(1,128)}), f32[64,1,2048]{2,1,0:T(1,128)S(1)}, u32[]{:S(2)}, u32[]{:S(2)}) %all-to-all-start.7) | async-done | bytes 524320 | tf_op jit(solution)/shard_map/all_to_all | solution.py:27
  (32 shorter events, 5.1 us)
Async XLA Ops:
  9.5 65.5 %all-to-all-start = ((bf16[1024,64,16]{0,2,1:T(8,128)(2,1)}), bf16[1024,64,16]{0,2,1:T(8,128)(2,1)S(1)}, u32[]{:S(2)}, u32[]{:S(2)}) async-start(bf16[1024,64,16]{0,2,1:T(8,128)(2,1)} %tile.2), calls=%async_computation | async-start | bytes 4194304 | tf_op jit(solution)/shard_map/all_to_all | solution.py:17
  22.7 155.4 %all-gather.2.cloned.1.call-start = ((), (), s32[]{:S(2)}) async-start(), calls=%async_computation.8 | async-start | bytes 2129920 | tf_op jit(solution)/shard_map/all_gather | solution.py:61
  79.5 1.9 copy-start
  158.6 31.6 %copy-start.1 = (bf16[1024,1024]{1,0:T(8,128)(2,1)S(1)}, bf16[1024,1024]{1,0:T(8,128)(2,1)}, u32[]{:S(2)}) copy-start(bf16[1024,1024]{1,0:T(8,128)(2,1)} %param.5) | copy-start | bytes 6291460
  170.6 19.4 %all-to-all-start.6 = ((f32[64,1,1024]{2,1,0:T(1,128)}), f32[64,1,1024]{2,1,0:T(1,128)S(1)}, u32[]{:S(2)}, u32[]{:S(2)}) async-start(f32[64,1,1024]{2,1,0:T(1,128)} %broadcast_in_dim.31), calls=%async_computation.6 | async-start | bytes 524288 | tf_op jit(solution)/shard_map/all_to_all | solution.py:27
  198.2 23.3 %all-to-all-start.7 = ((f32[64,1,2048]{2,1,0:T(1,128)}), f32[64,1,2048]{2,1,0:T(1,128)S(1)}, u32[]{:S(2)}, u32[]{:S(2)}) async-start(f32[64,1,2048]{2,1,0:T(1,128)} %broadcast_in_dim.32), calls=%async_computation.7 | async-start | bytes 1048576 | tf_op jit(solution)/shard_map/all_to_all | solution.py:27
Sparse Core Ops, SparseCore 0:
  26.2 81.1 all-gather.1
